TPU v7x, 32 devices: a 4x2x2 block of a 4x4x8 slice. The times are simulated.
32 devices in a mesh: data: 4 (over y, z), cp: 8 (over x, core).
Axes of the slice: x: 4, y: 2, z: 2, core: 2. Of those that a mesh axis runs over, the one named last changes fastest.
The devices are a block of a 4x4x8 slice.
Arguments:
- q: bfloat16 [32768, 4, 128], P(('data', 'cp')), parts along dimension 0
- k: bfloat16 [32768, 4, 128], P(('data', 'cp')), parts along dimension 0
- v: bfloat16 [32768, 4, 128], P(('data', 'cp')), parts along dimension 0
- o: bfloat16 [32768, 4, 128], P(('data', 'cp')), parts along dimension 0
- dout: bfloat16 [32768, 4, 128], P(('data', 'cp')), parts along dimension 0
- lse: float32 [4, 32768], P(None, ('data', 'cp')), parts along dimension 1
Outputs:
- output 1: bfloat16 [32768, 4, 128], P(('data', 'cp')), parts along dimension 0
- output 2: bfloat16 [32768, 4, 128], P(('data', 'cp')), parts along dimension 0
- output 3: bfloat16 [32768, 4, 128], P(('data', 'cp')), parts along dimension 0
There are 4 independent parts. A program takes and returns all parts, laid end to end along the dimension named above; each array names one.
All inputs are finite; a program needn't handle non-finite values.
Results may differ from a plain program's by a relative error of at most 0.001.
Values are sent between devices in bfloat16 or wider.
A program may use at most 768 MiB of HBM per device.

v0:
```python
import jax
import jax.numpy as jnp
from jax import lax
from jax.sharding import PartitionSpec as P

TILE = 512


def _tiles(q, dout, o, lse, n, me):
    c, h, d = q.shape
    m = c // TILE
    dd = jnp.einsum('qhd,qhd->hq', dout, o, preferred_element_type=jnp.float32)
    qpos = jnp.arange(c, dtype=jnp.int32) * n + me
    return (q.reshape(m, TILE, h, d), dout.reshape(m, TILE, h, d),
            lse.reshape(h, m, TILE).transpose(1, 0, 2),
            dd.reshape(h, m, TILE).transpose(1, 0, 2),
            qpos.reshape(m, TILE))


def _block_grads(xs, kb, vb, kpos, gk, gv, scale):
    f32 = jnp.float32

    def body(carry, x):
        gk, gv = carry
        qt, dt, lt, et, pt = x
        s = jnp.einsum('qhd,khd->hqk', qt, kb, preferred_element_type=f32) * scale
        mask = kpos[None, :] <= pt[:, None]
        p = jnp.where(mask[None], jnp.exp(s - lt[:, :, None]), 0.0)
        gv = gv + jnp.einsum('hqk,qhd->khd', p.astype(jnp.bfloat16), dt, preferred_element_type=f32)
        dp = jnp.einsum('qhd,khd->hqk', dt, vb, preferred_element_type=f32)
        ds = (p * (dp - et[:, :, None])).astype(jnp.bfloat16)
        dq = jnp.einsum('hqk,khd->qhd', ds, kb, preferred_element_type=f32) * scale
        gk = gk + jnp.einsum('hqk,qhd->khd', ds, qt, preferred_element_type=f32) * scale
        return (gk, gv), dq

    (gk, gv), dq = lax.scan(body, (gk, gv), xs)
    return dq, gk, gv


def solution(mesh):
    n = mesh.shape['cp']
    rows = P(('data', 'cp'))
    cols = P(None, ('data', 'cp'))
    perm = [(i, (i + 1) % n) for i in range(n)]

    def local(q, k, v, o, dout, lse):
        c, h, d = q.shape
        scale = d ** -0.5
        me = lax.axis_index('cp')
        xs = _tiles(q, dout, o, lse, n, me)
        base = jnp.arange(c, dtype=jnp.int32) * n
        dq = jnp.zeros((c // TILE, TILE, h, d), jnp.float32)
        gk = jnp.zeros((c, h, d), jnp.float32)
        gv = jnp.zeros((c, h, d), jnp.float32)
        kb, vb = k, v
        for s in range(n):
            kpos = base + (me - s) % n
            dqs, gk, gv = _block_grads(xs, kb, vb, kpos, gk, gv, scale)
            dq = dq + dqs
            if s < n - 1:
                kb = lax.ppermute(kb, 'cp', perm)
                vb = lax.ppermute(vb, 'cp', perm)
            gk = lax.ppermute(gk, 'cp', perm)
            gv = lax.ppermute(gv, 'cp', perm)
        return (dq.reshape(c, h, d).astype(jnp.bfloat16),
                gk.astype(jnp.bfloat16), gv.astype(jnp.bfloat16))

    return jax.shard_map(local, mesh=mesh, in_specs=(rows, rows, rows, rows, rows, cols),
                         out_specs=(rows, rows, rows), check_vma=False)
```

profile of v0, /device:TPU:88, one launch (start us, length us, event | category | flops | bytes accessed | tf_op | source)
XLA Modules:
  0.0 858.4 jit_solution(680302548718926103)
XLA Ops:
  11.0 41.8 %while.127 = (s32[]{:T(128)}, f32[1024,4,128]{0,2,1:T(8,128)}, f32[1024,4,128]{0,2,1:T(8,128)}, f32[2,512,4,128]{3,1,2,0:T(8,128)}, bf16[2,512,4,128]{3,1,2,0:T(...) while((s32[]{:T(128)}, f32[1024,4,128]{0,2,1:T(8,128)}, ...), condition=%wide.region_1.2_spmd.clone, body=%wide.region_0.1_spmd.clone.sunk | while | flops 2708736000 | bytes 146348896 | solution.py:36
  40.3 5.3 bitcast_add_fusion.46
  47.9 5.0 bitcast_add_fusion.47
  56.3 56.9 %collective-permute-done.2 = bf16[1024,4,128]{2,0,1:T(8,128)(2,1)} collective-permute-done((bf16[1024,4,128]{2,0,1:T(8,128)(2,1)S(1)}, bf16[1024,4,128]{2,0,1:T(8,128)(2,1)}, u32[]{:S(2)}, u32[]{:S(2)}) %collective-permute-start.2) | collective-permute-done | bytes 1048608 | tf_op jit(solution)/shard_map/ppermute | solution.py:61
  113.2 11.2 %collective-permute-done.3 = bf16[1024,4,128]{2,0,1:T(8,128)(2,1)} collective-permute-done((bf16[1024,4,128]{2,0,1:T(8,128)(2,1)}, bf16[1024,4,128]{2,0,1:T(8,128)(2,1)}, u32[]{:S(2)}, u32[]{:S(2)}) %collective-permute-start.3) | collective-permute-done | bytes 1048608 | tf_op jit(solution)/shard_map/ppermute | solution.py:62
  125.9 39.2 %while.120 = (s32[]{:T(128)}, f32[1024,4,128]{0,2,1:T(8,128)}, f32[1024,4,128]{0,2,1:T(8,128)}, f32[2,512,4,128]{3,1,2,0:T(8,128)}, bf16[2,512,4,128]{3,1,2,0:T(...) while((s32[]{:T(128)}, f32[1024,4,128]{0,2,1:T(8,128)}, ...), condition=%wide.region_3.4_spmd.clone, body=%wide.region_2.3_spmd.clone.sunk | while | flops 2707687424 | bytes 70850776 | solution.py:36
  167.4 58.1 %collective-permute-done.6 = bf16[1024,4,128]{2,0,1:T(8,128)(2,1)S(1)} collective-permute-done((bf16[1024,4,128]{2,0,1:T(8,128)(2,1)}, bf16[1024,4,128]{2,0,1:T(8,128)(2,1)S(1)}, u32[]{:S(2)}, u32[]{:S(2)}) %collective-permute-start.6) | collective-permute-done | bytes 1048608 | tf_op jit(solution)/shard_map/ppermute | solution.py:61
  225.5 11.2 %collective-permute-done.7 = bf16[1024,4,128]{2,0,1:T(8,128)(2,1)} collective-permute-done((bf16[1024,4,128]{2,0,1:T(8,128)(2,1)}, bf16[1024,4,128]{2,0,1:T(8,128)(2,1)}, u32[]{:S(2)}, u32[]{:S(2)}) %collective-permute-start.7) | collective-permute-done | bytes 1048608 | tf_op jit(solution)/shard_map/ppermute | solution.py:62
  238.4 34.5 %while.121 = (s32[]{:T(128)}, f32[1024,4,128]{0,2,1:T(8,128)}, f32[1024,4,128]{0,2,1:T(8,128)}, f32[2,512,4,128]{3,1,2,0:T(8,128)}, bf16[2,512,4,128]{3,1,2,0:T(...) while((s32[]{:T(128)}, f32[1024,4,128]{0,2,1:T(8,128)}, ...), condition=%wide.region_5.6_spmd.clone, body=%wide.region_4.5_spmd.clone.sunk | while | flops 2707687424 | bytes 70850776 | solution.py:36
  250.7 5.0 bitcast_add_fusion.35
  267.9 5.0 bitcast_add_fusion.35
  273.9 59.3 %collective-permute-done.10 = bf16[1024,4,128]{2,0,1:T(8,128)(2,1)} collective-permute-done((bf16[1024,4,128]{2,0,1:T(8,128)(2,1)S(1)}, bf16[1024,4,128]{2,0,1:T(8,128)(2,1)}, u32[]{:S(2)}, u32[]{:S(2)}) %collective-permute-start.10) | collective-permute-done | bytes 1048608 | tf_op jit(solution)/shard_map/ppermute | solution.py:61
  333.3 11.2 %collective-permute-done.11 = bf16[1024,4,128]{2,0,1:T(8,128)(2,1)} collective-permute-done((bf16[1024,4,128]{2,0,1:T(8,128)(2,1)}, bf16[1024,4,128]{2,0,1:T(8,128)(2,1)}, u32[]{:S(2)}, u32[]{:S(2)}) %collective-permute-start.11) | collective-permute-done | bytes 1048608 | tf_op jit(solution)/shard_map/ppermute | solution.py:62
  346.0 39.3 %while.122 = (s32[]{:T(128)}, f32[1024,4,128]{0,2,1:T(8,128)}, f32[1024,4,128]{0,2,1:T(8,128)}, f32[2,512,4,128]{3,1,2,0:T(8,128)}, bf16[2,512,4,128]{3,1,2,0:T(...) while((s32[]{:T(128)}, f32[1024,4,128]{0,2,1:T(8,128)}, ...), condition=%wide.region_7.8_spmd.clone, body=%wide.region_6.7_spmd.clone.sunk | while | flops 2707687424 | bytes 70850776 | solution.py:36
  385.4 60.2 %collective-permute-done.14 = bf16[1024,4,128]{2,0,1:T(8,128)(2,1)S(1)} collective-permute-done((bf16[1024,4,128]{2,0,1:T(8,128)(2,1)}, bf16[1024,4,128]{2,0,1:T(8,128)(2,1)S(1)}, u32[]{:S(2)}, u32[]{:S(2)}) %collective-permute-start.14) | collective-permute-done | bytes 1048608 | tf_op jit(solution)/shard_map/ppermute | solution.py:61
  445.6 11.2 %collective-permute-done.15 = bf16[1024,4,128]{2,0,1:T(8,128)(2,1)} collective-permute-done((bf16[1024,4,128]{2,0,1:T(8,128)(2,1)}, bf16[1024,4,128]{2,0,1:T(8,128)(2,1)}, u32[]{:S(2)}, u32[]{:S(2)}) %collective-permute-start.15) | collective-permute-done | bytes 1048608 | tf_op jit(solution)/shard_map/ppermute | solution.py:62
  458.3 34.6 %while.123 = (s32[]{:T(128)}, f32[1024,4,128]{0,2,1:T(8,128)}, f32[1024,4,128]{0,2,1:T(8,128)}, f32[2,512,4,128]{3,1,2,0:T(8,128)}, bf16[2,512,4,128]{3,1,2,0:T(...) while((s32[]{:T(128)}, f32[1024,4,128]{0,2,1:T(8,128)}, ...), condition=%wide.region_9.10_spmd.clone, body=%wide.region_8.9_spmd.clone.sunk | while | flops 2707687424 | bytes 70850776 | solution.py:36
  470.8 5.0 bitcast_add_fusion.39
  487.9 5.0 bitcast_add_fusion.39
  493.1 60.2 %collective-permute-done.18 = bf16[1024,4,128]{2,0,1:T(8,128)(2,1)} collective-permute-done((bf16[1024,4,128]{2,0,1:T(8,128)(2,1)S(1)}, bf16[1024,4,128]{2,0,1:T(8,128)(2,1)}, u32[]{:S(2)}, u32[]{:S(2)}) %collective-permute-start.18) | collective-permute-done | bytes 1048608 | tf_op jit(solution)/shard_map/ppermute | solution.py:61
  553.3 11.2 %collective-permute-done.19 = bf16[1024,4,128]{2,0,1:T(8,128)(2,1)} collective-permute-done((bf16[1024,4,128]{2,0,1:T(8,128)(2,1)}, bf16[1024,4,128]{2,0,1:T(8,128)(2,1)}, u32[]{:S(2)}, u32[]{:S(2)}) %collective-permute-start.19) | collective-permute-done | bytes 1048608 | tf_op jit(solution)/shard_map/ppermute | solution.py:62
  566.1 39.6 %while.124 = (s32[]{:T(128)}, f32[1024,4,128]{0,2,1:T(8,128)}, f32[1024,4,128]{0,2,1:T(8,128)}, f32[2,512,4,128]{3,1,2,0:T(8,128)}, bf16[2,512,4,128]{3,1,2,0:T(...) while((s32[]{:T(128)}, f32[1024,4,128]{0,2,1:T(8,128)}, ...), condition=%wide.region_11.12_spmd.clone, body=%wide.region_10.11_spmd.clone.sunk | while | flops 2707687424 | bytes 70850776 | solution.py:36
  605.8 60.2 %collective-permute-done.22 = bf16[1024,4,128]{2,0,1:T(8,128)(2,1)S(1)} collective-permute-done((bf16[1024,4,128]{2,0,1:T(8,128)(2,1)}, bf16[1024,4,128]{2,0,1:T(8,128)(2,1)S(1)}, u32[]{:S(2)}, u32[]{:S(2)}) %collective-permute-start.22) | collective-permute-done | bytes 1048608 | tf_op jit(solution)/shard_map/ppermute | solution.py:61
  666.0 11.2 %collective-permute-done.23 = bf16[1024,4,128]{2,0,1:T(8,128)(2,1)} collective-permute-done((bf16[1024,4,128]{2,0,1:T(8,128)(2,1)}, bf16[1024,4,128]{2,0,1:T(8,128)(2,1)}, u32[]{:S(2)}, u32[]{:S(2)}) %collective-permute-start.23) | collective-permute-done | bytes 1048608 | tf_op jit(solution)/shard_map/ppermute | solution.py:62
  678.8 34.5 %while.125 = (s32[]{:T(128)}, f32[1024,4,128]{0,2,1:T(8,128)}, f32[1024,4,128]{0,2,1:T(8,128)}, f32[2,512,4,128]{3,1,2,0:T(8,128)}, bf16[2,512,4,128]{3,1,2,0:T(...) while((s32[]{:T(128)}, f32[1024,4,128]{0,2,1:T(8,128)}, ...), condition=%wide.region_13.14_spmd.clone, body=%wide.region_12.13_spmd.clone.sunk | while | flops 2707687424 | bytes 70850776 | solution.py:36
  691.1 5.0 bitcast_add_fusion.43
  708.3 5.0 bitcast_add_fusion.43
  713.5 60.2 %collective-permute-done.26 = bf16[1024,4,128]{2,0,1:T(8,128)(2,1)} collective-permute-done((bf16[1024,4,128]{2,0,1:T(8,128)(2,1)S(1)}, bf16[1024,4,128]{2,0,1:T(8,128)(2,1)}, u32[]{:S(2)}, u32[]{:S(2)}) %collective-permute-start.26) | collective-permute-done | bytes 1048608 | tf_op jit(solution)/shard_map/ppermute | solution.py:61
  773.7 11.2 %collective-permute-done.27 = bf16[1024,4,128]{2,0,1:T(8,128)(2,1)} collective-permute-done((bf16[1024,4,128]{2,0,1:T(8,128)(2,1)}, bf16[1024,4,128]{2,0,1:T(8,128)(2,1)}, u32[]{:S(2)}, u32[]{:S(2)}) %collective-permute-start.27) | collective-permute-done | bytes 1048608 | tf_op jit(solution)/shard_map/ppermute | solution.py:62
  786.4 39.2 %while.126 = (s32[]{:T(128)}, f32[1024,4,128]{0,2,1:T(8,128)}, f32[1024,4,128]{0,2,1:T(8,128)}, f32[2,512,4,128]{3,1,2,0:T(8,128)}, bf16[2,512,4,128]{3,1,2,0:T(...) while((s32[]{:T(128)}, f32[1024,4,128]{0,2,1:T(8,128)}, ...), condition=%wide.region_15.16_spmd.clone, body=%wide.region_14.15_spmd.clone.sunk | while | flops 2707687424 | bytes 70850776 | solution.py:36
  830.8 6.3 add_convert_fusion
  843.4 11.2 %collective-permute-done.29 = bf16[1024,4,128]{2,1,0:T(4,128)(2,1)S(1)} collective-permute-done((bf16[1024,4,128]{2,1,0:T(4,128)(2,1)}, bf16[1024,4,128]{2,1,0:T(4,128)(2,1)S(1)}, u32[]{:S(2)}, u32[]{:S(2)}) %collective-permute-start.29) | collective-permute-done | bytes 1048608 | tf_op jit(solution)/shard_map/ppermute | solution.py:64
  (293 shorter events, 302.6 us)
Async XLA Ops:
  2.5 8.5 copy-start.20
  40.3 7.6 copy-start.2
  52.8 71.6 %collective-permute-start = (f32[1024,4,128]{0,2,1:T(8,128)}, f32[1024,4,128]{0,2,1:T(8,128)}, u32[]{:S(2)}, u32[]{:S(2)}) collective-permute-start(f32[1024,4,128]{0,2,1:T(8,128)} %get-tuple-element.516), channel_id=1, source_target_pairs={{0,1},{1,2},{2,3},{3,4},{4,5},{5,6},{6,7},{7,0},{8,9},{9,10},{10,1... | collective-permute-start | bytes 6291464 | tf_op jit(solution)/shard_map/ppermute | solution.py:63
  52.8 71.6 %collective-permute-start.1 = (f32[1024,4,128]{0,2,1:T(8,128)}, f32[1024,4,128]{0,2,1:T(8,128)}, u32[]{:S(2)}, u32[]{:S(2)}) collective-permute-start(f32[1024,4,128]{0,2,1:T(8,128)} %get-tuple-element.517), channel_id=1, source_target_pairs={{0,1},{1,2},{2,3},{3,4},{4,5},{5,6},{6,7},{7,0},{8,9},{9,10},{10,1... | collective-permute-start | bytes 6291464 | tf_op jit(solution)/shard_map/ppermute | solution.py:64
  54.6 58.6 %collective-permute-start.2 = (bf16[1024,4,128]{2,0,1:T(8,128)(2,1)S(1)}, bf16[1024,4,128]{2,0,1:T(8,128)(2,1)}, u32[]{:S(2)}, u32[]{:S(2)}) collective-permute-start(bf16[1024,4,128]{2,0,1:T(8,128)(2,1)S(1)} %get-tuple-element.2038), channel_id=1, source_target_pairs={{0,1},{1,2},{2,3},{3,4},{4,5},{5,6},{6,7},{7,0},{8,9},{9,10},{10,1... | collective-permute-start | bytes 3145736 | tf_op jit(solution)/shard_map/ppermute | solution.py:61
  54.6 69.9 %collective-permute-start.3 = (bf16[1024,4,128]{2,0,1:T(8,128)(2,1)}, bf16[1024,4,128]{2,0,1:T(8,128)(2,1)}, u32[]{:S(2)}, u32[]{:S(2)}) collective-permute-start(bf16[1024,4,128]{2,0,1:T(8,128)(2,1)} %get-tuple-element.2072), channel_id=1, source_target_pairs={{0,1},{1,2},{2,3},{3,4},{4,5},{5,6},{6,7},{7,0},{8,9},{9,10},{10,1... | collective-permute-start | bytes 3145736 | tf_op jit(solution)/shard_map/ppermute | solution.py:62
  165.1 71.6 %collective-permute-start.4 = (f32[1024,4,128]{0,2,1:T(8,128)}, f32[1024,4,128]{0,2,1:T(8,128)}, u32[]{:S(2)}, u32[]{:S(2)}) collective-permute-start(f32[1024,4,128]{0,2,1:T(8,128)} %get-tuple-element.519), channel_id=1, source_target_pairs={{0,1},{1,2},{2,3},{3,4},{4,5},{5,6},{6,7},{7,0},{8,9},{9,10},{10,1... | collective-permute-start | bytes 6291464 | tf_op jit(solution)/shard_map/ppermute | solution.py:63
  165.1 71.6 %collective-permute-start.5 = (f32[1024,4,128]{0,2,1:T(8,128)}, f32[1024,4,128]{0,2,1:T(8,128)}, u32[]{:S(2)}, u32[]{:S(2)}) collective-permute-start(f32[1024,4,128]{0,2,1:T(8,128)} %get-tuple-element.520), channel_id=1, source_target_pairs={{0,1},{1,2},{2,3},{3,4},{4,5},{5,6},{6,7},{7,0},{8,9},{9,10},{10,1... | collective-permute-start | bytes 6291464 | tf_op jit(solution)/shard_map/ppermute | solution.py:64
  165.7 59.9 %collective-permute-start.6 = (bf16[1024,4,128]{2,0,1:T(8,128)(2,1)}, bf16[1024,4,128]{2,0,1:T(8,128)(2,1)S(1)}, u32[]{:S(2)}, u32[]{:S(2)}) collective-permute-start(bf16[1024,4,128]{2,0,1:T(8,128)(2,1)} %collective-permute-done.2), channel_id=1, source_target_pairs={{0,1},{1,2},{2,3},{3,4},{4,5},{5,6},{6,7},{7,0},{8,9},{9,10},{10,1... | collective-permute-start | bytes 3145736 | tf_op jit(solution)/shard_map/ppermute | solution.py:61
  165.7 71.1 %collective-permute-start.7 = (bf16[1024,4,128]{2,0,1:T(8,128)(2,1)}, bf16[1024,4,128]{2,0,1:T(8,128)(2,1)}, u32[]{:S(2)}, u32[]{:S(2)}) collective-permute-start(bf16[1024,4,128]{2,0,1:T(8,128)(2,1)} %collective-permute-done.3), channel_id=1, source_target_pairs={{0,1},{1,2},{2,3},{3,4},{4,5},{5,6},{6,7},{7,0},{8,9},{9,10},{10,1... | collective-permute-start | bytes 3145736 | tf_op jit(solution)/shard_map/ppermute | solution.py:62
  272.9 71.6 %collective-permute-start.8 = (f32[1024,4,128]{0,2,1:T(8,128)}, f32[1024,4,128]{0,2,1:T(8,128)}, u32[]{:S(2)}, u32[]{:S(2)}) collective-permute-start(f32[1024,4,128]{0,2,1:T(8,128)} %get-tuple-element.522), channel_id=1, source_target_pairs={{0,1},{1,2},{2,3},{3,4},{4,5},{5,6},{6,7},{7,0},{8,9},{9,10},{10,1... | collective-permute-start | bytes 6291464 | tf_op jit(solution)/shard_map/ppermute | solution.py:63
  272.9 71.6 %collective-permute-start.9 = (f32[1024,4,128]{0,2,1:T(8,128)}, f32[1024,4,128]{0,2,1:T(8,128)}, u32[]{:S(2)}, u32[]{:S(2)}) collective-permute-start(f32[1024,4,128]{0,2,1:T(8,128)} %get-tuple-element.523), channel_id=1, source_target_pairs={{0,1},{1,2},{2,3},{3,4},{4,5},{5,6},{6,7},{7,0},{8,9},{9,10},{10,1... | collective-permute-start | bytes 6291464 | tf_op jit(solution)/shard_map/ppermute | solution.py:64
  272.9 60.4 %collective-permute-start.10 = (bf16[1024,4,128]{2,0,1:T(8,128)(2,1)S(1)}, bf16[1024,4,128]{2,0,1:T(8,128)(2,1)}, u32[]{:S(2)}, u32[]{:S(2)}) collective-permute-start(bf16[1024,4,128]{2,0,1:T(8,128)(2,1)S(1)} %get-tuple-element.2044), channel_id=1, source_target_pairs={{0,1},{1,2},{2,3},{3,4},{4,5},{5,6},{6,7},{7,0},{8,9},{9,10},{10,1... | collective-permute-start | bytes 3145736 | tf_op jit(solution)/shard_map/ppermute | solution.py:61
  273.0 71.5 %collective-permute-start.11 = (bf16[1024,4,128]{2,0,1:T(8,128)(2,1)}, bf16[1024,4,128]{2,0,1:T(8,128)(2,1)}, u32[]{:S(2)}, u32[]{:S(2)}) collective-permute-start(bf16[1024,4,128]{2,0,1:T(8,128)(2,1)} %collective-permute-done.7), channel_id=1, source_target_pairs={{0,1},{1,2},{2,3},{3,4},{4,5},{5,6},{6,7},{7,0},{8,9},{9,10},{10,1... | collective-permute-start | bytes 3145736 | tf_op jit(solution)/shard_map/ppermute | solution.py:62
  385.3 71.6 %collective-permute-start.12 = (f32[1024,4,128]{0,2,1:T(8,128)}, f32[1024,4,128]{0,2,1:T(8,128)}, u32[]{:S(2)}, u32[]{:S(2)}) collective-permute-start(f32[1024,4,128]{0,2,1:T(8,128)} %get-tuple-element.525), channel_id=1, source_target_pairs={{0,1},{1,2},{2,3},{3,4},{4,5},{5,6},{6,7},{7,0},{8,9},{9,10},{10,1... | collective-permute-start | bytes 6291464 | tf_op jit(solution)/shard_map/ppermute | solution.py:63
  385.3 71.6 %collective-permute-start.13 = (f32[1024,4,128]{0,2,1:T(8,128)}, f32[1024,4,128]{0,2,1:T(8,128)}, u32[]{:S(2)}, u32[]{:S(2)}) collective-permute-start(f32[1024,4,128]{0,2,1:T(8,128)} %get-tuple-element.526), channel_id=1, source_target_pairs={{0,1},{1,2},{2,3},{3,4},{4,5},{5,6},{6,7},{7,0},{8,9},{9,10},{10,1... | collective-permute-start | bytes 6291464 | tf_op jit(solution)/shard_map/ppermute | solution.py:64
  385.3 60.4 %collective-permute-start.14 = (bf16[1024,4,128]{2,0,1:T(8,128)(2,1)}, bf16[1024,4,128]{2,0,1:T(8,128)(2,1)S(1)}, u32[]{:S(2)}, u32[]{:S(2)}) collective-permute-start(bf16[1024,4,128]{2,0,1:T(8,128)(2,1)} %collective-permute-done.10), channel_id=1, source_target_pairs={{0,1},{1,2},{2,3},{3,4},{4,5},{5,6},{6,7},{7,0},{8,9},{9,10},{10,1... | collective-permute-start | bytes 3145736 | tf_op jit(solution)/shard_map/ppermute | solution.py:61
  385.3 71.5 %collective-permute-start.15 = (bf16[1024,4,128]{2,0,1:T(8,128)(2,1)}, bf16[1024,4,128]{2,0,1:T(8,128)(2,1)}, u32[]{:S(2)}, u32[]{:S(2)}) collective-permute-start(bf16[1024,4,128]{2,0,1:T(8,128)(2,1)} %collective-permute-done.11), channel_id=1, source_target_pairs={{0,1},{1,2},{2,3},{3,4},{4,5},{5,6},{6,7},{7,0},{8,9},{9,10},{10,1... | collective-permute-start | bytes 3145736 | tf_op jit(solution)/shard_map/ppermute | solution.py:62
  493.0 71.6 %collective-permute-start.16 = (f32[1024,4,128]{0,2,1:T(8,128)}, f32[1024,4,128]{0,2,1:T(8,128)}, u32[]{:S(2)}, u32[]{:S(2)}) collective-permute-start(f32[1024,4,128]{0,2,1:T(8,128)} %get-tuple-element.528), channel_id=1, source_target_pairs={{0,1},{1,2},{2,3},{3,4},{4,5},{5,6},{6,7},{7,0},{8,9},{9,10},{10,1... | collective-permute-start | bytes 6291464 | tf_op jit(solution)/shard_map/ppermute | solution.py:63
  493.0 71.6 %collective-permute-start.17 = (f32[1024,4,128]{0,2,1:T(8,128)}, f32[1024,4,128]{0,2,1:T(8,128)}, u32[]{:S(2)}, u32[]{:S(2)}) collective-permute-start(f32[1024,4,128]{0,2,1:T(8,128)} %get-tuple-element.529), channel_id=1, source_target_pairs={{0,1},{1,2},{2,3},{3,4},{4,5},{5,6},{6,7},{7,0},{8,9},{9,10},{10,1... | collective-permute-start | bytes 6291464 | tf_op jit(solution)/shard_map/ppermute | solution.py:64
  493.0 60.4 %collective-permute-start.18 = (bf16[1024,4,128]{2,0,1:T(8,128)(2,1)S(1)}, bf16[1024,4,128]{2,0,1:T(8,128)(2,1)}, u32[]{:S(2)}, u32[]{:S(2)}) collective-permute-start(bf16[1024,4,128]{2,0,1:T(8,128)(2,1)S(1)} %get-tuple-element.2047), channel_id=1, source_target_pairs={{0,1},{1,2},{2,3},{3,4},{4,5},{5,6},{6,7},{7,0},{8,9},{9,10},{10,1... | collective-permute-start | bytes 3145736 | tf_op jit(solution)/shard_map/ppermute | solution.py:61
  493.0 71.5 %collective-permute-start.19 = (bf16[1024,4,128]{2,0,1:T(8,128)(2,1)}, bf16[1024,4,128]{2,0,1:T(8,128)(2,1)}, u32[]{:S(2)}, u32[]{:S(2)}) collective-permute-start(bf16[1024,4,128]{2,0,1:T(8,128)(2,1)} %collective-permute-done.15), channel_id=1, source_target_pairs={{0,1},{1,2},{2,3},{3,4},{4,5},{5,6},{6,7},{7,0},{8,9},{9,10},{10,1... | collective-permute-start | bytes 3145736 | tf_op jit(solution)/shard_map/ppermute | solution.py:62
  605.7 71.6 %collective-permute-start.20 = (f32[1024,4,128]{0,2,1:T(8,128)}, f32[1024,4,128]{0,2,1:T(8,128)}, u32[]{:S(2)}, u32[]{:S(2)}) collective-permute-start(f32[1024,4,128]{0,2,1:T(8,128)} %get-tuple-element.531), channel_id=1, source_target_pairs={{0,1},{1,2},{2,3},{3,4},{4,5},{5,6},{6,7},{7,0},{8,9},{9,10},{10,1... | collective-permute-start | bytes 6291464 | tf_op jit(solution)/shard_map/ppermute | solution.py:63
  605.7 71.6 %collective-permute-start.21 = (f32[1024,4,128]{0,2,1:T(8,128)}, f32[1024,4,128]{0,2,1:T(8,128)}, u32[]{:S(2)}, u32[]{:S(2)}) collective-permute-start(f32[1024,4,128]{0,2,1:T(8,128)} %get-tuple-element.532), channel_id=1, source_target_pairs={{0,1},{1,2},{2,3},{3,4},{4,5},{5,6},{6,7},{7,0},{8,9},{9,10},{10,1... | collective-permute-start | bytes 6291464 | tf_op jit(solution)/shard_map/ppermute | solution.py:64
  605.7 60.4 %collective-permute-start.22 = (bf16[1024,4,128]{2,0,1:T(8,128)(2,1)}, bf16[1024,4,128]{2,0,1:T(8,128)(2,1)S(1)}, u32[]{:S(2)}, u32[]{:S(2)}) collective-permute-start(bf16[1024,4,128]{2,0,1:T(8,128)(2,1)} %collective-permute-done.18), channel_id=1, source_target_pairs={{0,1},{1,2},{2,3},{3,4},{4,5},{5,6},{6,7},{7,0},{8,9},{9,10},{10,1... | collective-permute-start | bytes 3145736 | tf_op jit(solution)/shard_map/ppermute | solution.py:61
  605.7 71.5 %collective-permute-start.23 = (bf16[1024,4,128]{2,0,1:T(8,128)(2,1)}, bf16[1024,4,128]{2,0,1:T(8,128)(2,1)}, u32[]{:S(2)}, u32[]{:S(2)}) collective-permute-start(bf16[1024,4,128]{2,0,1:T(8,128)(2,1)} %collective-permute-done.19), channel_id=1, source_target_pairs={{0,1},{1,2},{2,3},{3,4},{4,5},{5,6},{6,7},{7,0},{8,9},{9,10},{10,1... | collective-permute-start | bytes 3145736 | tf_op jit(solution)/shard_map/ppermute | solution.py:62
  713.3 71.6 %collective-permute-start.24 = (f32[1024,4,128]{0,2,1:T(8,128)}, f32[1024,4,128]{0,2,1:T(8,128)}, u32[]{:S(2)}, u32[]{:S(2)}) collective-permute-start(f32[1024,4,128]{0,2,1:T(8,128)} %get-tuple-element.534), channel_id=1, source_target_pairs={{0,1},{1,2},{2,3},{3,4},{4,5},{5,6},{6,7},{7,0},{8,9},{9,10},{10,1... | collective-permute-start | bytes 6291464 | tf_op jit(solution)/shard_map/ppermute | solution.py:63
  713.3 71.6 %collective-permute-start.25 = (f32[1024,4,128]{0,2,1:T(8,128)}, f32[1024,4,128]{0,2,1:T(8,128)}, u32[]{:S(2)}, u32[]{:S(2)}) collective-permute-start(f32[1024,4,128]{0,2,1:T(8,128)} %get-tuple-element.535), channel_id=1, source_target_pairs={{0,1},{1,2},{2,3},{3,4},{4,5},{5,6},{6,7},{7,0},{8,9},{9,10},{10,1... | collective-permute-start | bytes 6291464 | tf_op jit(solution)/shard_map/ppermute | solution.py:64
  713.3 60.4 %collective-permute-start.26 = (bf16[1024,4,128]{2,0,1:T(8,128)(2,1)S(1)}, bf16[1024,4,128]{2,0,1:T(8,128)(2,1)}, u32[]{:S(2)}, u32[]{:S(2)}) collective-permute-start(bf16[1024,4,128]{2,0,1:T(8,128)(2,1)S(1)} %get-tuple-element.2041), channel_id=1, source_target_pairs={{0,1},{1,2},{2,3},{3,4},{4,5},{5,6},{6,7},{7,0},{8,9},{9,10},{10,1... | collective-permute-start | bytes 3145736 | tf_op jit(solution)/shard_map/ppermute | solution.py:61
  713.4 71.5 %collective-permute-start.27 = (bf16[1024,4,128]{2,0,1:T(8,128)(2,1)}, bf16[1024,4,128]{2,0,1:T(8,128)(2,1)}, u32[]{:S(2)}, u32[]{:S(2)}) collective-permute-start(bf16[1024,4,128]{2,0,1:T(8,128)(2,1)} %collective-permute-done.23), channel_id=1, source_target_pairs={{0,1},{1,2},{2,3},{3,4},{4,5},{5,6},{6,7},{7,0},{8,9},{9,10},{10,1... | collective-permute-start | bytes 3145736 | tf_op jit(solution)/shard_map/ppermute | solution.py:62
  827.9 15.5 %collective-permute-start.28 = (bf16[1024,4,128]{2,1,0:T(4,128)(2,1)S(1)}, bf16[1024,4,128]{2,1,0:T(4,128)(2,1)}, u32[]{:S(2)}, u32[]{:S(2)}) collective-permute-start(bf16[1024,4,128]{2,1,0:T(4,128)(2,1)S(1)} %copy.71), channel_id=1, source_target_pairs={{0,1},{1,2},{2,3},{3,4},{4,5},{5,6},{6,7},{7,0},{8,9},{9,10},{10,1... | collective-permute-start | bytes 3145736 | tf_op jit(solution)/shard_map/ppermute | solution.py:63
  830.8 23.9 %collective-permute-start.29 = (bf16[1024,4,128]{2,1,0:T(4,128)(2,1)}, bf16[1024,4,128]{2,1,0:T(4,128)(2,1)S(1)}, u32[]{:S(2)}, u32[]{:S(2)}) collective-permute-start(bf16[1024,4,128]{2,1,0:T(4,128)(2,1)} %copy.72), channel_id=1, source_target_pairs={{0,1},{1,2},{2,3},{3,4},{4,5},{5,6},{6,7},{7,0},{8,9},{9,10},{10,1... | collective-permute-start | bytes 3145736 | tf_op jit(solution)/shard_map/ppermute | solution.py:64
  (42 other events, 181.1 us)
where the time goes:
time: 867 us; the launch traced here: 858 us
  waiting for transfers between devices  510 us (59%)
  matrix products  287 us (33%)
  local copies, waits for them, and re-layouts  35.9 us (4%)
  other arithmetic  14.1 us (2%)
    ppermute x7, waiting for transfers between devices, local(): kb = lax.ppermute(kb, 'cp', perm)  415 us
    ppermute x7, waiting for transfers between devices, local(): vb = lax.ppermute(vb, 'cp', perm)  78.6 us
    dot_general x16, matrix products, body(): jnp.einsum('hqk,qhd->khd', p.astype(jnp.bfloat16), dt, preferred_element_...  78.4 us
    dot_general x16, matrix products, body(): jnp.einsum('hqk,qhd->khd', ds, qt, preferred_element_type=f32) * scale  75.1 us
    dot_general x16, matrix products, body(): dp = jnp.einsum('qhd,khd->hqk', dt, vb, preferred_element_type=f32)  71.8 us
    dot_general x16, matrix products, body(): dq = jnp.einsum('hqk,khd->qhd', ds, kb, preferred_element_type=f32) * scale  32.1 us
    dot_general x16, matrix products, body(): s = jnp.einsum('qhd,khd->hqk', qt, kb, preferred_element_type=f32) * scale  29.8 us
  transfers between devices with their start and end apart: 30, of which 16 were waited for; matrix products, arithmetic and copies ran while one was open for 1% of the time, Pallas kernels for 0%

commit v1 on v0

v1 whole, which is shorter than its diff:
```python
import functools

import jax
import jax.numpy as jnp
from jax import lax
from jax.experimental import pallas as pl
from jax.experimental.pallas import tpu as pltpu
from jax.sharding import PartitionSpec as P

TB = 64
LOG2E = 1.4426950408889634
MESH = pl.DeviceIdType.MESH
NN = (((1,), (0,)), ((), ()))
NT = (((1,), (1,)), ((), ()))
TN = (((0,), (0,)), ((), ()))


def _dot(a, b, dims):
    return lax.dot_general(a, b, dims, preferred_element_type=jnp.float32)


def _kernel(n, scale, q_ref, k_ref, v_ref, do_ref, ld_ref, oq_ref, ok_ref, ov_ref,
            qx, dox, kx, vx, ldx, lseb, db, rel, dq, dqr, dk, dv, dqo, dko, dvo,
            s_in, r_in, s_ld, r_ld, s_fw, r_fw, s_dq, r_dq, s_out, r_out):
    f32, bf16 = jnp.float32, jnp.bfloat16
    me = lax.axis_index('cp')
    x, c = lax.div(me, 2), lax.rem(me, 2)
    sib = x * 2 + (1 - c)
    ni = kx.shape[0]
    blk = n * TB
    d = q_ref.shape[-1]
    split = ni - 2

    def own(core, i):
        return 2 * i + lax.rem(core + i, 2)

    def rows(b):
        return pl.ds(pl.multiple_of(b * TB, TB), TB)

    def copy(src, dst, s, r, dev):
        return pltpu.make_async_remote_copy(src_ref=src, dst_ref=dst, send_sem=s, recv_sem=r,
                                            device_id={'cp': dev}, device_id_type=MESH)

    bar = pltpu.get_barrier_semaphore()
    for t in range(1, n):
        pl.semaphore_signal(bar, 1, device_id={'cp': lax.rem(me + t, n)}, device_id_type=MESH)
    pl.semaphore_wait(bar, n - 1)

    def send_ld(t, _):
        to = lax.rem(me + t, n)
        copy(ld_ref.at[lax.div(to, 2)], ldx.at[me], s_ld, r_ld, to).start()
        return 0

    lax.fori_loop(1, n, send_ld, 0)
    ins = ((q_ref, qx), (do_ref, dox), (k_ref, kx), (v_ref, vx))

    def send_block(i, _):
        def to_dev(t, _):
            to = lax.rem(me + t, n)
            h, b = lax.div(to, 2), own(lax.rem(to, 2), i)
            for a, (src, dst) in enumerate(ins):
                copy(src.at[h, rows(b)], dst.at[b if a < 2 else i, me], s_in.at[a], r_in.at[i, a], to).start()
            return 0
        lax.fori_loop(1, n, to_dev, 0)
        return 0

    lax.fori_loop(0, ni, send_block, 0)

    def keep(i, _):
        b = own(c, i)
        qx[b, me] = q_ref[x, rows(b)]
        dox[b, me] = do_ref[x, rows(b)]
        kx[i, me] = k_ref[x, rows(b)]
        vx[i, me] = v_ref[x, rows(b)]
        return 0

    lax.fori_loop(0, ni, keep, 0)
    ldx[me] = ld_ref[x]

    def zero(i, _):
        dk[i] = jnp.zeros((blk, d), f32)
        dv[i] = jnp.zeros((blk, d), f32)
        dq[2 * i] = jnp.zeros((blk, d), f32)
        dq[2 * i + 1] = jnp.zeros((blk, d), f32)
        return 0

    lax.fori_loop(0, ni, zero, 0)

    def rel_rows(j, _):
        tt = lax.broadcasted_iota(jnp.int32, (TB, 2 * blk), 0)
        ql = lax.broadcasted_iota(jnp.int32, (TB, 2 * blk), 1)
        l2 = lax.rem(ql, blk)
        qpos = (ql - l2) + lax.rem(l2, TB) * n + lax.div(l2, TB)
        rel[rows(j)] = tt * n + j - qpos
        return 0

    lax.fori_loop(0, n, rel_rows, 0)

    def wait_in(i):
        for a in range(4):
            part = kx.at[0, pl.ds(0, n - 1)]
            copy(part, part, s_in.at[a], r_in.at[i, a], sib).wait_recv()

    def forward(i):
        b = own(c, i)
        copy(qx.at[b], qx.at[b], s_fw.at[0], r_fw.at[i, 0], sib).start()
        copy(dox.at[b], dox.at[b], s_fw.at[1], r_fw.at[i, 1], sib).start()

    def wait_forward(i):
        for a in range(2):
            copy(kx.at[0], kx.at[0], s_fw.at[a], r_fw.at[i, a], sib).wait_recv()

    wait_in(0)
    forward(0)
    part = ldx.at[pl.ds(0, n - 1)]
    copy(part, part, s_ld, r_ld, sib).wait_recv()
    low = lax.broadcasted_iota(jnp.int32, (ni, 2 * TB), 1) < TB
    for m in range(n // 2):
        for w, dst, f in ((0, lseb, LOG2E), (1, db, 1.0)):
            a, b = ldx[2 * m, w] * f, ldx[2 * m + 1, w] * f
            dst[:, pl.ds(m * 2 * TB, 2 * TB)] = jnp.where(low, a, pltpu.roll(b, TB, 1))
            dst[:, pl.ds(blk + m * 2 * TB, 2 * TB)] = jnp.where(low, pltpu.roll(a, TB, 1), b)

    def tile(i, p, masked):
        q = qx[pl.ds(2 * p, 2)].reshape(2 * blk, d)
        do = dox[pl.ds(2 * p, 2)].reshape(2 * blk, d)
        k = kx[i].reshape(blk, d)
        v = vx[i].reshape(blk, d)
        s = _dot(k, q, NT)
        pr = jnp.exp2(s * (scale * LOG2E) - lseb[pl.ds(p, 1), :])
        if masked:
            pr = jnp.where(rel[...] <= -blk * lax.rem(c + i, 2), pr, 0.0)
        dv[i] += _dot(pr.astype(bf16), do, NN)
        dp = _dot(v, do, NT)
        ds = (pr * (dp - db[pl.ds(p, 1), :])).astype(bf16)
        dk[i] += _dot(ds, q, NN)
        dq[pl.ds(2 * p, 2)] += _dot(ds, k, TN).reshape(2, blk, d)

    def either(i, p):
        @pl.when(i < p)
        def _():
            tile(i, p, False)

        @pl.when(i == p)
        def _():
            tile(i, p, True)

    def dq_swap(p):
        copy(dq.at[own(1 - c, p)], dqr.at[p], s_dq, r_dq.at[p], sib).start()

    def dq_join(p):
        copy(dqr.at[0], dqr.at[0], s_dq, r_dq.at[p], sib).wait_recv()
        g = ((dq[own(c, p)] + dqr[p]) * scale).astype(bf16)
        dqo[p] = g.reshape(n, TB, d)

    def send_out(src, dst, a, i):
        b = own(c, i)

        def to_dev(t, _):
            to = lax.rem(me + t, n)
            copy(src.at[i, to], dst.at[x, rows(b)], s_out.at[a], r_out.at[a], to).start()
            return 0

        lax.fori_loop(1, n, to_dev, 0)
        dst[x, rows(b)] = src[i, me]

    def dq_send(p):
        send_out(dqo, oq_ref, 0, p)

    def kv_round(i):
        dko[i] = (dk[i] * scale).astype(bf16).reshape(n, TB, d)
        dvo[i] = dv[i].astype(bf16).reshape(n, TB, d)

    def kv_send(i):
        send_out(dko, ok_ref, 1, i)
        send_out(dvo, ov_ref, 2, i)

    def row(p, _):
        wait_forward(p)

        def step(i, _):
            @pl.when(i == p)
            def _():
                wait_in(p + 1)
                forward(p + 1)

            either(i, p)

            @pl.when((i == 0) & (p >= 1))
            def _():
                dq_swap(p - 1)

            @pl.when((i == 0) & (p >= 2))
            def _():
                dq_send(p - 2)
            return 0

        lax.fori_loop(0, p + 1, step, 0)

        @pl.when(p >= 1)
        def _():
            dq_join(p - 1)
        return 0

    lax.fori_loop(0, split, row, 0)

    wait_forward(split)
    wait_in(split + 1)
    forward(split + 1)

    def column(i, _):
        @pl.when(i <= split)
        def _():
            either(i, split)

        @pl.when(i == 0)
        def _():
            dq_swap(split - 1)
            dq_send(split - 2)
            wait_forward(split + 1)

        @pl.when(i >= 1)
        def _():
            kv_send(i - 1)

        @pl.when(i == 1)
        def _():
            dq_send(split - 1)

        either(i, split + 1)

        @pl.when(i == 0)
        def _():
            dq_join(split - 1)

        @pl.when(i == split)
        def _():
            dq_swap(split)

        kv_round(i)
        return 0

    lax.fori_loop(0, ni, column, 0)
    dq_swap(split + 1)
    dq_join(split)
    kv_send(ni - 1)
    dq_join(split + 1)
    dq_send(split)
    dq_send(split + 1)

    part = kx.at[pl.ds(0, n - 1)]
    for a in range(3):
        copy(part, part, s_out.at[a], r_out.at[a], sib).wait()
    for a in range(4):
        copy(part, part, s_in.at[a], r_out.at[0], sib).wait_send()
    for a in range(2):
        copy(kx, kx, s_fw.at[a], r_out.at[0], sib).wait_send()
    copy(dqr, dqr, s_dq, r_out.at[0], sib).wait_send()
    part = ldx.at[pl.ds(0, n - 1)]
    copy(part, part, s_ld, r_out.at[0], sib).wait_send()


def solution(mesh):
    n = mesh.shape['cp']
    rows = P(('data', 'cp'))
    cols = P(None, ('data', 'cp'))

    def local(q, k, v, o, dout, lse):
        c, h, d = q.shape
        assert 2 * h == n and d == 2 * TB and c % (2 * TB) == 0 and n * TB % 128 == 0
        ni = c // (2 * TB)
        blk = n * TB
        f32, bf16 = jnp.float32, jnp.bfloat16
        dd = jnp.einsum('qhd,qhd->hq', dout, o, preferred_element_type=f32)
        ld = jnp.stack([lse, dd], axis=1).reshape(h, 2, ni, 2 * TB)
        heads = [a.transpose(1, 0, 2) for a in (q, k, v, dout)]
        vm = pl.BlockSpec(memory_space=pltpu.VMEM)
        dma = pltpu.SemaphoreType.DMA
        outs = pl.pallas_call(
            functools.partial(_kernel, n, d ** -0.5),
            out_shape=[jax.ShapeDtypeStruct((h, c, d), bf16)] * 3,
            in_specs=[vm] * 5,
            out_specs=[vm] * 3,
            scratch_shapes=[
                pltpu.VMEM((2 * ni, n, TB, d), bf16),
                pltpu.VMEM((2 * ni, n, TB, d), bf16),
                pltpu.VMEM((ni, n, TB, d), bf16),
                pltpu.VMEM((ni, n, TB, d), bf16),
                pltpu.VMEM((n, 2, ni, 2 * TB), f32),
                pltpu.VMEM((ni, 2 * blk), f32),
                pltpu.VMEM((ni, 2 * blk), f32),
                pltpu.VMEM((blk, 2 * blk), jnp.int32),
                pltpu.VMEM((2 * ni, blk, d), f32),
                pltpu.VMEM((ni, blk, d), f32),
                pltpu.VMEM((ni, blk, d), f32),
                pltpu.VMEM((ni, blk, d), f32),
                pltpu.VMEM((ni, n, TB, d), bf16),
                pltpu.VMEM((ni, n, TB, d), bf16),
                pltpu.VMEM((ni, n, TB, d), bf16),
                dma((4,)), dma((ni, 4)), dma, dma, dma((2,)), dma((ni, 2)), dma, dma((ni,)), dma((3,)), dma((3,)),
            ],
            compiler_params=pltpu.CompilerParams(collective_id=0, has_side_effects=True,
                                                 vmem_limit_bytes=60 * 2 ** 20),
            name='attention_grads',
        )(heads[0], heads[1], heads[2], heads[3], ld)
        return tuple(a.transpose(1, 0, 2) for a in outs)

    return jax.shard_map(local, mesh=mesh, in_specs=(rows, rows, rows, rows, rows, cols),
                         out_specs=(rows, rows, rows), check_vma=False)
```

time: 867 us -> 116 us (0.13)
  the two profiles are of different devices: /device:TPU:88 before, /device:TPU:81 now
where the time goes in v1:
time: 116 us; the launch traced here: 115 us
  Pallas kernels  99.7 us (86%)
  local copies, waits for them, and re-layouts  11.5 us (10%)
  other arithmetic  3.5 us (3%)
    pallas_call x1, Pallas kernels, local(): pl.pallas_call(functools.partial(_kernel, n, d ** (-0.5)), out_shape=[jax...  99.7 us
    unnamed x16, local copies, waits for them, and re-layouts  8.09 us
    transpose x2, local copies, waits for them, and re-layouts, local(): heads = [a.transpose(1, 0, 2) for a in (q, k, v, dout)]  3.18 us
    unnamed x1, other arithmetic  2.87 us

profile of v1, /device:TPU:81, one launch (start us, length us, event | category | flops | bytes accessed | tf_op | source)
XLA Modules:
  0.0 115.4 jit_solution(16696183082538156775)
XLA Ops:
  0.6 0.7 copy.31
  1.4 0.0 copy-start.3
  1.4 0.0 copy-start.4
  1.4 2.9 %fusion = f32[4,1024]{0,1:T(8,128)S(1)} fusion(bf16[1024,4,128]{2,1,0:T(4,128)(2,1)} %param.9, bf16[1024,4,128]{2,1,0:T(4,128)(2,1)} %param.10), kind=kLoop, calls=%fused_computation.1 | loop fusion | flops 2093056 | bytes 2113536
  4.2 0.2 copy.24
  4.4 0.6 pad_maximum_fusion.ld_ref
  5.0 0.0 copy-done.3
  5.0 0.0 copy-done.4
  5.0 0.0 copy-start
  5.1 0.0 copy-start.5
  5.1 1.6 %copy_bitcast_fusion.2 = (bf16[4,1024,128]{2,1,0:T(8,128)(2,1)}, bf16[4,1024,128]{2,1,0:T(8,128)(2,1)}) fusion(bf16[1024,4,128]{2,1,0:T(4,128)(2,1)S(1)} %copy-done.3, bf16[1024,4,128]{2,1,0:T(4,128)(2,1)S(1)} %copy-done.4), kind=kLoop, calls=%fused_computation.4 | loop fusion | bytes 4194304 | tf_op jit(solution)/shard_map/transpose | solution.py:276
  6.6 0.0 copy-done
  6.7 0.7 copy-done.5
  7.3 1.6 %copy_bitcast_fusion = (bf16[4,1024,128]{2,1,0:T(8,128)(2,1)}, bf16[4,1024,128]{2,1,0:T(8,128)(2,1)}) fusion(bf16[1024,4,128]{2,1,0:T(4,128)(2,1)S(1)} %copy-done, bf16[1024,4,128]{2,1,0:T(4,128)(2,1)S(1)} %copy-done.5), kind=kLoop, calls=%fused_computation.2 | loop fusion | bytes 4194304 | tf_op jit(solution)/shard_map/transpose | solution.py:276
  8.9 99.7 %attention_grads.1 = (bf16[4,1024,128]{2,1,0:T(8,128)(2,1)}, bf16[4,1024,128]{2,1,0:T(8,128)(2,1)}, bf16[4,1024,128]{2,1,0:T(8,128)(2,1)}) custom-call(bf16[4,1024,128]{2,1,0:T(8,128)(2,1)} %get-tuple-element.15.q_ref, bf16[4,1024,128]{2,1,0:T(8,128)(2,1)} %get-tuple-element.14.k_ref, bf16[4,1024,128]{2,1,0:T(8,128)(2,1)} %get-tuple-element.13.v_ref, ...), custom_call_target="tpu_custom_call" | custom-call | tf_op jit(solution)/shard_map/attention_grads/pallas_call | solution.py:279
  108.7 0.0 copy-start.2
  108.7 3.1 %copy.13 = bf16[1024,4,128]{2,1,0:T(4,128)(2,1)} copy(bf16[1024,4,128]{2,0,1:T(8,128)(2,1)} %bitcast.24) | data formatting | bytes 2097152
  111.8 0.0 copy-done.2
  111.8 0.0 copy-start.1
  111.8 1.8 %copy.14 = bf16[1024,4,128]{2,1,0:T(4,128)(2,1)} copy(bf16[1024,4,128]{2,0,1:T(8,128)(2,1)S(1)} %bitcast.23) | data formatting | bytes 2097152
  113.6 0.0 copy-done.1
  113.6 1.8 %copy.15 = bf16[1024,4,128]{2,1,0:T(4,128)(2,1)} copy(bf16[1024,4,128]{2,0,1:T(8,128)(2,1)S(1)} %bitcast.22) | data formatting | bytes 2097152
Async XLA Ops:
  1.4 3.7 %copy-start.3 = (bf16[1024,4,128]{2,1,0:T(4,128)(2,1)S(1)}, bf16[1024,4,128]{2,1,0:T(4,128)(2,1)}, u32[]{:S(2)}) copy-start(bf16[1024,4,128]{2,1,0:T(4,128)(2,1)} %param.7) | copy-start | bytes 3145732
  1.4 3.7 %copy-start.4 = (bf16[1024,4,128]{2,1,0:T(4,128)(2,1)S(1)}, bf16[1024,4,128]{2,1,0:T(4,128)(2,1)}, u32[]{:S(2)}) copy-start(bf16[1024,4,128]{2,1,0:T(4,128)(2,1)} %param.6) | copy-start | bytes 3145732
  5.0 1.6 %copy-start = (bf16[1024,4,128]{2,1,0:T(4,128)(2,1)S(1)}, bf16[1024,4,128]{2,1,0:T(4,128)(2,1)}, u32[]{:S(2)}) copy-start(bf16[1024,4,128]{2,1,0:T(4,128)(2,1)} %param.10) | copy-start | bytes 3145732
  5.1 2.3 %copy-start.5 = (bf16[1024,4,128]{2,1,0:T(4,128)(2,1)S(1)}, bf16[1024,4,128]{2,1,0:T(4,128)(2,1)}, u32[]{:S(2)}) copy-start(bf16[1024,4,128]{2,1,0:T(4,128)(2,1)} %param.8) | copy-start | bytes 3145732
  108.7 3.1 %copy-start.2 = (bf16[4,1024,128]{2,1,0:T(8,128)(2,1)S(1)}, bf16[4,1024,128]{2,1,0:T(8,128)(2,1)}, u32[]{:S(2)}) copy-start(bf16[4,1024,128]{2,1,0:T(8,128)(2,1)} %get-tuple-element.7) | copy-start | bytes 3145732
  111.8 1.8 %copy-start.1 = (bf16[4,1024,128]{2,1,0:T(8,128)(2,1)S(1)}, bf16[4,1024,128]{2,1,0:T(8,128)(2,1)}, u32[]{:S(2)}) copy-start(bf16[4,1024,128]{2,1,0:T(8,128)(2,1)} %get-tuple-element.8) | copy-start | bytes 3145732

commit v2 on v1

v2 whole, which is shorter than its diff:
```python
import functools

import jax
import jax.numpy as jnp
from jax import lax
from jax.experimental import pallas as pl
from jax.experimental.pallas import tpu as pltpu
from jax.sharding import PartitionSpec as P

TB = 64
LOG2E = 1.4426950408889634
MESH = pl.DeviceIdType.MESH
NN = (((1,), (0,)), ((), ()))
NT = (((1,), (1,)), ((), ()))


def _dot(a, b, dims):
    return lax.dot_general(a, b, dims, preferred_element_type=jnp.float32)


def _kernel(n, heads, scale, q_hbm, do_hbm, k_hbm, v_hbm, lse_ref, dd_ref, gq_hbm, gk_hbm, gv_hbm,
            inb, tmp, snd, ld, qx, dox, kx, vx, kt, ldx, ldb, rel, dq, dqr, dk, dv, dqo, dko, dvo, land,
            s_load, s_in, r_in, s_fw, r_fw, s_dq, r_dq, s_out, r_out, s_own):
    f32, bf16 = jnp.float32, jnp.bfloat16
    me = lax.axis_index('cp')
    x, c = lax.div(me, 2), lax.rem(me, 2)
    sib = x * 2 + (1 - c)
    ni = kx.shape[0]
    blk = n * TB
    d = q_hbm.shape[-1]
    split = ni - 2
    pr_rows = 2 * TB
    chunk = pr_rows * heads

    def own(core, i):
        return 2 * i + lax.rem(core + i, 2)

    def rows(b):
        return pl.ds(pl.multiple_of(b * TB, TB), TB)

    def span(i, size):
        return pl.ds(pl.multiple_of(i * size, size), size)

    def copy(src, dst, s, r, dev):
        return pltpu.make_async_remote_copy(src_ref=src, dst_ref=dst, send_sem=s, recv_sem=r,
                                            device_id={'cp': dev}, device_id_type=MESH)

    srcs = (q_hbm, do_hbm, k_hbm, v_hbm)

    def load(p):
        return [pltpu.make_async_copy(src.at[span(p, chunk)], inb.at[a, p], s_load.at[a, p])
                for a, src in enumerate(srcs)]

    def start_load(p, _):
        for cp in load(p):
            cp.start()
        return 0

    lax.fori_loop(0, ni, start_load, 0)

    bar = pltpu.get_barrier_semaphore()
    for t in range(1, n):
        pl.semaphore_signal(bar, 1, device_id={'cp': lax.rem(me + t, n)}, device_id_type=MESH)
    pl.semaphore_wait(bar, n - 1)

    def widen(p):
        for cp in load(p):
            cp.wait()
        for a in range(4):
            tmp[lax.rem(p, 2), a] = inb[a, p].astype(f32)

    def arrange(p):
        for h in range(heads):
            for a in range(4):
                snd[a, h, span(p, pr_rows)] = tmp[lax.rem(p, 2), a, pl.ds(h, pr_rows, stride=heads), :].astype(bf16)
            ld[h, p, 0:1] = lse_ref[pl.ds(h, 1), span(p, pr_rows)] * LOG2E
            ld[h, p, 1:2] = dd_ref[pl.ds(h, 1), span(p, pr_rows)]

    ins = (qx, dox, kx, vx)

    def send_block(i):
        def to_dev(t, _):
            to = lax.rem(me + t, n)
            h, b = lax.div(to, 2), own(lax.rem(to, 2), i)
            copy(ld.at[h, i], ldx.at[me, i], s_in.at[4], r_in.at[i, 4], to).start()
            for a, dst in enumerate(ins):
                copy(snd.at[a, h, rows(b)], dst.at[b if a < 2 else i, me], s_in.at[a], r_in.at[i, a], to).start()
            return 0
        lax.fori_loop(1, n, to_dev, 0)

    widen(0)
    widen(1)
    arrange(0)

    def feed(i, _):
        @pl.when(i < ni - 2)
        def _():
            widen(i + 2)

        @pl.when(i < ni - 1)
        def _():
            arrange(i + 1)

        send_block(i)
        return 0

    lax.fori_loop(0, ni, feed, 0)

    def keep(i, _):
        b = own(c, i)
        qx[b, me] = snd[0, x, rows(b)]
        dox[b, me] = snd[1, x, rows(b)]
        kx[i, me] = snd[2, x, rows(b)]
        vx[i, me] = snd[3, x, rows(b)]
        return 0

    lax.fori_loop(0, ni, keep, 0)
    ldx[me] = ld[x]

    def zero(i, _):
        dk[i] = jnp.zeros((blk, d), f32)
        dv[i] = jnp.zeros((blk, d), f32)
        dq[2 * i] = jnp.zeros((d, blk), f32)
        dq[2 * i + 1] = jnp.zeros((d, blk), f32)
        return 0

    lax.fori_loop(0, ni, zero, 0)

    def rel_rows(j, _):
        tt = lax.broadcasted_iota(jnp.int32, (TB, blk), 0)
        ql = lax.broadcasted_iota(jnp.int32, (TB, blk), 1)
        rel[rows(j)] = tt * n + j - lax.rem(ql, TB) * n - lax.div(ql, TB)
        return 0

    lax.fori_loop(0, n, rel_rows, 0)

    def wait_in(i):
        for a in range(4):
            part = kx.at[0, pl.ds(0, n - 1)]
            copy(part, part, s_in.at[a], r_in.at[i, a], sib).wait_recv()
        part = ldx.at[pl.ds(0, n - 1), 0]
        copy(part, part, s_in.at[4], r_in.at[i, 4], sib).wait_recv()

    low = lax.broadcasted_iota(jnp.int32, (2, pr_rows), 1) < TB

    def forward(i):
        b = own(c, i)
        copy(qx.at[b], qx.at[b], s_fw.at[0], r_fw.at[i, 0], sib).start()
        copy(dox.at[b], dox.at[b], s_fw.at[1], r_fw.at[i, 1], sib).start()
        kt[i] = kx[i].reshape(blk, d).astype(f32).T.astype(bf16)
        for m in range(n // 2):
            a, b = ldx[2 * m, i], ldx[2 * m + 1, i]
            ldb[i, :, pl.ds(m * pr_rows, pr_rows)] = jnp.where(low, a, pltpu.roll(b, TB, 1))
            ldb[i, :, pl.ds(blk + m * pr_rows, pr_rows)] = jnp.where(low, pltpu.roll(a, TB, 1), b)

    def wait_forward(i):
        for a in range(2):
            copy(kx.at[0], kx.at[0], s_fw.at[a], r_fw.at[i, a], sib).wait_recv()

    wait_in(0)
    forward(0)

    def tile(i, p, half, nb, masked):
        b = 2 * p + half
        q = qx[pl.ds(b, nb)].reshape(nb * blk, d)
        do = dox[pl.ds(b, nb)].reshape(nb * blk, d)
        cols = span(half, blk) if nb == 1 else slice(None)
        s = _dot(kx[i].reshape(blk, d), q, NT)
        pr = jnp.exp2(s * (scale * LOG2E) - ldb[p, 0:1, cols])
        if masked:
            pr = jnp.where(rel[...] <= 0, pr, 0.0)
        dv[i] += _dot(pr.astype(bf16), do, NN)
        dp = _dot(vx[i].reshape(blk, d), do, NT)
        ds = (pr * (dp - ldb[p, 1:2, cols])).astype(bf16)
        dk[i] += _dot(ds, q, NN)
        g = _dot(kt[i], ds, NN)
        for m in range(nb):
            dq[b + m] += g[:, m * blk:(m + 1) * blk]

    def either(i, p):
        off = lax.rem(c + i, 2)

        @pl.when(i < p)
        def _():
            tile(i, p, 0, 2, False)

        @pl.when(i == p)
        def _():
            tile(i, p, off, 1, True)

        @pl.when((i == p) & (off == 0))
        def _():
            tile(i, p, 1, 1, False)

    def dq_swap(p):
        copy(dq.at[own(1 - c, p)], dqr.at[p], s_dq, r_dq.at[p], sib).start()

    def dq_join(p):
        copy(dqr.at[0], dqr.at[0], s_dq, r_dq.at[p], sib).wait_recv()
        g = (dq[own(c, p)] + dqr[p]) * scale
        dqo[p] = g.T.astype(bf16).reshape(n, TB, d)

    outs = (gq_hbm, gk_hbm, gv_hbm)

    def send_out(src, a, i):
        b = own(c, i)

        def to_dev(t, _):
            to = lax.rem(me + t, n)
            copy(src.at[i, to], land.at[a, x, rows(b)], s_out.at[a], r_out.at[a, i], to).start()
            return 0

        lax.fori_loop(1, n, to_dev, 0)
        land[a, x, rows(b)] = src[i, me]

    def dq_send(p):
        send_out(dqo, 0, p)

    def kv_round(i):
        dko[i] = (dk[i] * scale).astype(bf16).reshape(n, TB, d)
        dvo[i] = dv[i].astype(bf16).reshape(n, TB, d)

    def kv_send(i):
        send_out(dko, 1, i)
        send_out(dvo, 2, i)

    def row(p, _):
        wait_forward(p)

        def step(i, _):
            @pl.when(i == p)
            def _():
                wait_in(p + 1)
                forward(p + 1)

            either(i, p)

            @pl.when((i == 0) & (p >= 1))
            def _():
                dq_swap(p - 1)

            @pl.when((i == 0) & (p >= 2))
            def _():
                dq_send(p - 2)
            return 0

        lax.fori_loop(0, p + 1, step, 0)

        @pl.when(p >= 1)
        def _():
            dq_join(p - 1)
        return 0

    lax.fori_loop(0, split, row, 0)

    wait_forward(split)
    wait_in(split + 1)
    forward(split + 1)

    def column(i, _):
        @pl.when(i <= split)
        def _():
            either(i, split)

        @pl.when(i == 0)
        def _():
            dq_swap(split - 1)
            dq_send(split - 2)
            wait_forward(split + 1)

        @pl.when((i >= 1) & (i <= split))
        def _():
            kv_send(i - 1)

        @pl.when(i == 1)
        def _():
            dq_send(split - 1)

        either(i, split + 1)

        @pl.when(i == 0)
        def _():
            dq_join(split - 1)

        @pl.when(i == split)
        def _():
            dq_swap(split)

        @pl.when(i > split)
        def _():
            kv_send(i - 1)

        kv_round(i)
        return 0

    lax.fori_loop(0, ni, column, 0)
    dq_swap(split + 1)
    dq_join(split)
    kv_send(ni - 1)
    dq_join(split + 1)
    dq_send(split)
    dq_send(split + 1)

    def leave(a, p):
        return pltpu.make_async_copy(land.at[a, :, span(p, pr_rows)], outs[a].at[:, span(p, pr_rows)], s_own.at[a, p])

    def finish(a, p):
        part = kx.at[0, pl.ds(0, n - 1)]
        copy(part, part, s_out.at[a], r_out.at[a, p], sib).wait_recv()
        leave(a, p).start()

    def finish_q(p, _):
        finish(0, p)
        return 0

    def finish_kv(p, _):
        finish(1, p)
        finish(2, p)
        return 0

    lax.fori_loop(0, split, finish_q, 0)
    lax.fori_loop(0, ni, finish_kv, 0)
    lax.fori_loop(split, ni, finish_q, 0)

    part = kx.at[pl.ds(0, n - 1)]
    for a in range(3):
        copy(part, part, s_out.at[a], r_out.at[0, 0], sib).wait_send()
    for a in range(4):
        copy(part, part, s_in.at[a], r_out.at[0, 0], sib).wait_send()
    for a in range(2):
        copy(kx, kx, s_fw.at[a], r_out.at[0, 0], sib).wait_send()
    copy(dqr, dqr, s_dq, r_out.at[0, 0], sib).wait_send()
    part = ldx.at[pl.ds(0, n - 1)]
    copy(part, part, s_in.at[4], r_out.at[0, 0], sib).wait_send()

    def left(p, _):
        for a in range(3):
            leave(a, p).wait()
        return 0

    lax.fori_loop(0, ni, left, 0)


def _merge_kernel(heads, steps, a_hbm, b_hbm, c_hbm, x_hbm, y_hbm, z_hbm, vin, vout, tmp, s_in, s_out):
    size = vin.shape[2] // steps
    parts = [(a, r) for r in range(steps) for a in range(3)]

    def load(a, r):
        rows = pl.ds(r * size, size)
        return pltpu.make_async_copy((a_hbm, b_hbm, c_hbm)[a].at[:, rows], vin.at[a, :, rows], s_in.at[a, r])

    def store(a, r):
        rows = pl.ds(r * size * heads, size * heads)
        return pltpu.make_async_copy(vout.at[a, rows], (x_hbm, y_hbm, z_hbm)[a].at[rows], s_out.at[a, r])

    for a, r in parts:
        load(a, r).start()
    last = len(parts)
    for j in range(last + 2):
        if j < last:
            a, r = parts[j]
            load(a, r).wait()
            for h in range(heads):
                tmp[j % 2, pl.ds(h, size, stride=heads), :] = vin[a, h, pl.ds(r * size, size)].astype(jnp.float32)
        if 0 < j <= last:
            a, r = parts[j - 1]
            vout[a, pl.ds(r * size * heads, size * heads)] = tmp[(j - 1) % 2].astype(vout.dtype)
        if j > 1:
            store(*parts[j - 2]).start()
    for a, r in parts:
        store(a, r).wait()


def solution(mesh):
    n = mesh.shape['cp']
    rows = P(('data', 'cp'))
    cols = P(None, ('data', 'cp'))

    def local(q, k, v, o, dout, lse):
        c, h, d = q.shape
        assert 2 * h == n and d == 2 * TB and c % (2 * TB) == 0 and n * TB % 128 == 0
        ni = c // (2 * TB)
        blk = n * TB
        chunk = 2 * TB * h
        f32, bf16 = jnp.float32, jnp.bfloat16
        flat = [a.reshape(c * h, d) for a in (q, dout, k, v)]
        dd = jnp.einsum('qhd,qhd->hq', dout, o, preferred_element_type=f32)
        vmem, dma = pltpu.VMEM, pltpu.SemaphoreType.DMA
        hbm = pl.BlockSpec(memory_space=pl.ANY)
        outs = pl.pallas_call(
            functools.partial(_kernel, n, h, d ** -0.5),
            out_shape=[jax.ShapeDtypeStruct((h, c, d), bf16)] * 3,
            in_specs=[hbm] * 4 + [pl.BlockSpec(memory_space=vmem)] * 2,
            out_specs=[hbm] * 3,
            scratch_shapes=[
                vmem((4, ni, chunk, d), bf16),
                vmem((2, 4, chunk, d), f32),
                vmem((4, h, c, d), bf16),
                vmem((h, ni, 2, 2 * TB), f32),
                vmem((2 * ni, n, TB, d), bf16),
                vmem((2 * ni, n, TB, d), bf16),
                vmem((ni, n, TB, d), bf16),
                vmem((ni, n, TB, d), bf16),
                vmem((ni, d, blk), bf16),
                vmem((n, ni, 2, 2 * TB), f32),
                vmem((ni, 2, 2 * blk), f32),
                vmem((blk, blk), jnp.int32),
                vmem((2 * ni, d, blk), f32),
                vmem((ni, d, blk), f32),
                vmem((ni, blk, d), f32),
                vmem((ni, blk, d), f32),
                vmem((ni, n, TB, d), bf16),
                vmem((ni, n, TB, d), bf16),
                vmem((ni, n, TB, d), bf16),
                vmem((3, h, c, d), bf16),
                dma((4, ni)), dma((5,)), dma((ni, 5)), dma((2,)), dma((ni, 2)), dma, dma((ni,)),
                dma((3,)), dma((3, ni)), dma((3, ni)),
            ],
            compiler_params=pltpu.CompilerParams(collective_id=0, has_side_effects=True,
                                                 vmem_limit_bytes=60 * 2 ** 20),
            name='attention_grads',
        )(*flat, lse, dd)
        steps = 4
        outs = pl.pallas_call(
            functools.partial(_merge_kernel, h, steps),
            out_shape=[jax.ShapeDtypeStruct((c * h, d), bf16)] * 3,
            in_specs=[hbm] * 3,
            out_specs=[hbm] * 3,
            scratch_shapes=[vmem((3, h, c, d), bf16), vmem((3, c * h, d), bf16), vmem((2, c // steps * h, d), f32),
                            dma((3, steps)), dma((3, steps))],
            compiler_params=pltpu.CompilerParams(vmem_limit_bytes=60 * 2 ** 20),
            name='merge_heads',
        )(*outs)
        return tuple(a.reshape(c, h, d) for a in outs)

    return jax.shard_map(local, mesh=mesh, in_specs=(rows, rows, rows, rows, rows, cols),
                         out_specs=(rows, rows, rows), check_vma=False)
```

time: 116 us -> 102 us (0.88)
  local copies, waits for them, and re-layouts: 11.5 us -> 0.79 us
  Pallas kernels: 99.7 us -> 97.4 us
    unnamed x16 -> x0, local copies, waits for them, and re-layouts: 8.09 us -> none
    transpose x2 -> x0, local copies, waits for them, and re-layouts: 3.18 us -> none  [local(): heads = [a.transpose(1, 0, 2) for a in (q, k, v, dout)]]
    pallas_call x1 -> x2, Pallas kernels: 99.7 us -> 97.4 us  [the longest x1 94.3 us: local(): pl.pallas_call(functools.partial(_kernel, n, h, d ** (-0.5)), out_shape=[...]
where the time goes in v2:
time: 102 us
  Pallas kernels  97.4 us (95%)
  other arithmetic  2.73 us (3%)
    pallas_call x1, Pallas kernels, local(): pl.pallas_call(functools.partial(_kernel, n, h, d ** (-0.5)), out_shape=[...  94.3 us
    pallas_call x1, Pallas kernels, local(): pl.pallas_call(functools.partial(_merge_kernel, h, steps), out_shape=[jax...  3.1 us
    unnamed x1, other arithmetic  2.73 us

profile of v2, /device:TPU:81, one launch (start us, length us, event | category | flops | bytes accessed | tf_op | source)
XLA Modules:
  0.0 101.5 jit_solution(8248456650153362273)
XLA Ops:
  0.6 2.7 %fusion = f32[4,1024]{0,1:T(8,128)S(1)} fusion(bf16[1024,4,128]{2,1,0:T(4,128)(2,1)} %param.9, bf16[1024,4,128]{2,1,0:T(4,128)(2,1)} %param.10), kind=kLoop, calls=%fused_computation.1 | loop fusion | flops 2093056 | bytes 2113536
  3.4 0.8 copy.15.dd_ref
  4.2 94.3 %attention_grads.1 = (bf16[4,1024,128]{2,1,0:T(8,128)(2,1)}, bf16[4,1024,128]{2,1,0:T(8,128)(2,1)}, bf16[4,1024,128]{2,1,0:T(8,128)(2,1)}) custom-call(bf16[4096,128]{1,0:T(8,128)(2,1)} %bitcast.12, bf16[4096,128]{1,0:T(8,128)(2,1)} %bitcast.11, bf16[4096,128]{1,0:T(8,128)(2,1)} %bitcast.13, bf16[4096,128]{1,0:T(8,128)(2,1)} %bitcast.14, f32[4,1024]{1,0:T(4,128)} %lse_ref.1, ...), custom_call_target="tpu_custom_call" | custom-call | tf_op jit(solution)/shard_map/attention_grads/pallas_call | solution.py:390
  98.4 3.1 %merge_heads.1 = (bf16[4096,128]{1,0:T(8,128)(2,1)}, bf16[4096,128]{1,0:T(8,128)(2,1)}, bf16[4096,128]{1,0:T(8,128)(2,1)}) custom-call(bf16[4,1024,128]{2,1,0:T(8,128)(2,1)} %get-tuple-element.9.a_hbm, bf16[4,1024,128]{2,1,0:T(8,128)(2,1)} %get-tuple-element.10.b_hbm, bf16[4,1024,128]{2,1,0:T(8,128)(2,1)} %get-tuple-element.11.c_hbm), custom_call_target="tpu_custom_call" | custom-call | tf_op jit(solution)/shard_map/merge_heads/pallas_call | solution.py:424
